TPU v7x, 256 devices: a whole 4x4x8 slice. The times are simulated.
256 devices in a mesh: dp: 8 (over z), expert: 32 (over x, y, core).
Axes of the slice: x: 4, y: 4, z: 8, core: 2. Of those that a mesh axis runs over, the one named last changes fastest.
Arguments:
- tokens: bfloat16 [65536, 2048], P(('dp', 'expert')), may hold values from -6 to 6
- expert_ranks: int32 [32, 65536], P(None, ('dp', 'expert')), may hold values from 0 to 65535, as said below
- capacity: int32 [32], replicated, may hold values from 512 to 1024, as said below
- weight_in: bfloat16 [32, 2048, 8192], P('expert', None, 'dp'), may hold values from -0.125 to 0.125
- weight_out: bfloat16 [32, 8192, 2048], P('expert', 'dp'), may hold values from -0.0625 to 0.0625
- gate_weights: float32 [32, 1024], P('expert', 'dp'), may hold values from 0.05 to 1
Outputs:
- combined: bfloat16 [65536, 2048], P(('dp', 'expert'))
Inputs may be any that keep to these rules, and one draw needn't show every extreme that they name: `expert_ranks`: for each expert the ranks are a permutation of 0 to 65535. Of the 256 tokens of one device, at most 8 have rank under 1024 for one expert; for an expert of capacity 1024, some devices have exactly 8. At least one expert has capacity 1024.
All inputs are finite; a program needn't handle non-finite values.
Results may differ from a plain program's by a relative error of at most 0.0053.
Values may be sent and summed in bfloat16 or wider, within the bound.
No kernel may reach another device: no remote copies, remote signals or barrier semaphores. Data moves between devices by JAX's collectives and lax.ppermute only.
A program may use at most 64 MiB of HBM per device.

v0:
```python
import jax
import jax.numpy as jnp
from jax import lax
from jax.sharding import Mesh
from jax.sharding import PartitionSpec as P

MOST = 8
LANES = 128
EXPERT = ("expert_0", "expert_1", "expert_2")
DP_EXPERT = ("dp", "expert_0", "expert_1", "expert_2")


def exclusive(values):
    return jnp.cumsum(values) - values


def on_device(tokens, expert_ranks, capacity, weight_in, weight_out, gate_weights):
    dp_count = lax.axis_size("dp")
    expert_count = lax.axis_size(EXPERT)
    token_count, width = tokens.shape
    slots_dp = gate_weights.shape[1]
    rows_all = expert_count * MOST
    own_dp = lax.axis_index("dp")
    own_expert = lax.axis_index(EXPERT)
    chosen = expert_ranks < capacity[:, None]
    chosen_int = chosen.astype(jnp.int32)
    counts = jnp.sum(chosen_int, axis=1)
    before = jnp.cumsum(chosen_int, axis=1) - chosen_int
    places = lax.broadcasted_iota(jnp.int32, (expert_count, MOST, token_count), 1)
    pack_table = jnp.logical_and(chosen[:, None, :], before[:, None, :] == places)
    pack_table = pack_table.astype(jnp.bfloat16).reshape(rows_all, token_count)
    packed = jnp.dot(pack_table, tokens, preferred_element_type=jnp.float32).astype(jnp.bfloat16)
    arrived_rows = lax.all_to_all(
        packed.reshape(expert_count, MOST, width), EXPERT, split_axis=0, concat_axis=0, tiled=True
    ).reshape(rows_all, width)
    device_ids = lax.broadcasted_iota(jnp.int32, (expert_count, expert_count), 0)
    expert_ids = lax.broadcasted_iota(jnp.int32, (expert_count, expert_count), 1)
    table = jnp.where(device_ids == own_expert, counts[None, :], 0)
    table = lax.psum(table.reshape(-1, LANES), EXPERT).reshape(expert_count, expert_count)
    arrived = jnp.sum(jnp.where(expert_ids == own_expert, table, 0), axis=1)
    plane_ids = lax.broadcasted_iota(jnp.int32, (dp_count, LANES), 0)
    lane_ids = lax.broadcasted_iota(jnp.int32, (dp_count, LANES), 1)
    plane_row = jnp.pad(jnp.sum(table, axis=0).astype(jnp.float32), (0, LANES - expert_count))
    both = jnp.concatenate(
        [
            jnp.where(plane_ids == own_dp, plane_row[None, :], 0.0),
            jnp.where(plane_ids == own_dp, gate_weights.reshape(-1, LANES), 0.0),
        ]
    )
    both = lax.psum(both, "dp")
    plane_counts = both[:dp_count].astype(jnp.int32)
    most_rows = jnp.max(plane_counts)
    earlier = jnp.logical_and(plane_ids < own_dp, lane_ids == own_expert)
    first_slot = jnp.sum(jnp.where(earlier, plane_counts, 0))
    gates_all = jnp.concatenate([both[dp_count:].reshape(-1), jnp.zeros((rows_all,), jnp.float32)])
    within = lax.broadcasted_iota(jnp.int32, (expert_count, MOST), 1)
    target = jnp.where(within < arrived[:, None], exclusive(arrived)[:, None] + within, -1).reshape(
        rows_all
    )

    def experts(rows, plane_rows):
        slot_ids = lax.broadcasted_iota(jnp.int32, (rows_all, plane_rows), 1)
        place_table = (target[:, None] == slot_ids).astype(jnp.bfloat16)
        plane = lax.dot_general(
            place_table, rows, (((0,), (0,)), ((), ())), preferred_element_type=jnp.float32
        ).astype(jnp.bfloat16)
        slot_rows = lax.all_gather(plane, "dp", axis=0, tiled=True)
        hidden = jnp.maximum(
            jnp.dot(slot_rows, weight_in[0], preferred_element_type=jnp.float32), 0.0
        ).astype(jnp.bfloat16)
        share = jnp.dot(hidden, weight_out[0], preferred_element_type=jnp.float32)
        out = lax.psum_scatter(
            share.astype(jnp.bfloat16), "dp", scatter_dimension=0, tiled=True
        ).astype(jnp.float32)
        gates = lax.dynamic_slice_in_dim(gates_all, first_slot, plane_rows, 0)
        scaled = (gates[:, None] * out).astype(jnp.bfloat16)
        returned = jnp.dot(place_table, scaled, preferred_element_type=jnp.float32)
        return returned.astype(jnp.bfloat16)

    fair = slots_dp + slots_dp // 4
    sent_back = lax.cond(
        most_rows <= fair,
        lambda rows: experts(rows, fair),
        lambda rows: experts(rows, rows_all),
        arrived_rows,
    )
    results = lax.all_to_all(
        sent_back.reshape(expert_count, MOST, width),
        EXPERT,
        split_axis=0,
        concat_axis=0,
        tiled=True,
    ).reshape(rows_all, width)
    combined = lax.dot_general(
        pack_table, results, (((0,), (0,)), ((), ())), preferred_element_type=jnp.float32
    )
    return combined.astype(jnp.bfloat16)


def solution(mesh):
    split = Mesh(
        mesh.devices.reshape(mesh.shape["dp"], 4, 4, 2), ("dp", "expert_0", "expert_1", "expert_2")
    )
    placed = (
        P(DP_EXPERT, None),
        P(None, DP_EXPERT),
        P(),
        P(EXPERT, None, "dp"),
        P(EXPERT, "dp", None),
        P(EXPERT, "dp"),
    )
    return jax.shard_map(
        on_device, mesh=split, in_specs=placed, out_specs=P(DP_EXPERT, None), check_vma=False
    )
```

profile of v0, /device:TPU:1, one launch (start us, length us, event | category | flops | bytes accessed | tf_op | source)
XLA Modules:
  0.0 348.8 jit_solution(17893966849262882347)
XLA Ops:
  6.5 0.9 convert_bitcast_fusion.1
  7.5 0.6 reduce-window.18
  8.1 0.2 slice_reduce_fusion
  8.3 0.1 iota.90
  8.4 0.1 convert_subtract_fusion
  8.5 1.5 fusion.19
  10.0 8.6 %all-to-all-start = ((bf16[32,8,2048]{2,1,0:T(8,128)(2,1)}), bf16[32,8,2048]{2,1,0:T(8,128)(2,1)S(1)}, u32[]{:S(2)}, u32[]{:S(2)}) async-start(bf16[32,8,2048]{2,1,0:T(8,128)(2,1)} %fusion.19), calls=%async_computation.2 | async-start | bytes 2097152 | tf_op jit(solution)/shard_map/all_to_all | solution.py:33
  18.7 0.1 iota.80
  18.9 127.0 %psum.14 = s32[32,32]{1,0:T(8,128)S(1)} all-reduce(s32[32,32]{1,0:T(8,128)S(1)} %reshape.73), channel_id=1, replica_groups=mesh['dp'=8,'expert_0'=4,'expert_1'=4,'expert_2'=2] {'expert_0','expert_..., use_global_device_ids=true, to_apply=%region_3.4 | all-reduce | flops 1024 | bytes 8192 | tf_op jit(solution)/shard_map/psum | solution.py:39
  145.9 0.1 select_reduce_fusion
  146.1 16.5 %psum.15 = f32[16,128]{1,0:T(8,128)S(1)} all-reduce(f32[16,128]{1,0:T(8,128)S(1)} %pad_maximum_fusion), channel_id=1, replica_groups=mesh['dp'=8,'expert_0'=4,'expert_1'=4,'expert_2'=2] {'dp'}, use_global_device_ids=true, to_apply=%region_5.6 | all-reduce | flops 2048 | bytes 16384 | tf_op jit(solution)/shard_map/psum | solution.py:50
  162.7 0.8 select_reduce_fusion.1
  164.2 0.1 copy.19
  164.3 0.1 reduce.1
  164.5 151.7 %conditional.2 = (bf16[256,2048]{1,0:T(8,128)(2,1)S(1)}) conditional(s32[]{:T(128)} %convert_element_type.61, (s32[32,8]{1,0:T(8,128)S(1)}, s32[]{:T(128)}, f32[1280]{0:T(1024)S(1)}, bf16[256,2048]{1,0:T(8,128)(2,1)S(1)}, bf16[1,2048,1024]{2,1,0:T(8,128)(2,1)}, /*index=5*/bf16[1,1024,2048]{2,1,0:T(8,128)(2,1)}) %tuple.30, (s32[32,8]{1,0:T(8,128)S(1)}, ...), branch_computations={%region_10.12_spmd, %region_12.14_spmd} | conditional | flops 17727356928 | bytes 85990520
  164.6 0.1 eq.49
  164.7 1.3 convolution_convert_fusion.3
  166.0 0.2 reduce-scatter.5.cloned.1.call-start
  166.2 67.1 %all-gather.5.cloned.1.call-done = bf16[1280,2048]{1,0:T(8,128)(2,1)} async-done(((bf16[160,2048]{1,0:T(8,128)(2,1)}), bf16[1280,2048]{1,0:T(8,128)(2,1)}) %all-gather.5.cloned.1.call-update) | async-done | bytes 5242896 | tf_op jit(solution)/shard_map/cond/branch_1_fun/all_gather | solution.py:67
  233.4 16.9 %convolution_convert_fusion.2 = bf16[1280,2048]{1,0:T(8,128)(2,1)} fusion(bf16[1,1024,2048]{2,1,0:T(8,128)(2,1)} %get-tuple-element.45, bf16[1280,2048]{1,0:T(8,128)(2,1)} %all-gather.5.cloned.1.call-done, bf16[1,2048,1024]{2,1,0:T(8,128)(2,1)} %get-tuple-element.44), kind=kOutput, calls=%fused_computation.13 | convolution fusion | flops 10742661120 | bytes 18874368 | tf_op jit(solution)/shard_map/cond/branch_1_fun/dot_general | solution.py:71
  252.0 62.3 %reduce-scatter.5.cloned.1.call-done = bf16[160,2048]{1,0:T(8,128)(2,1)} async-done(((bf16[1280,2048]{1,0:T(8,128)(2,1)}), bf16[160,2048]{1,0:T(8,128)(2,1)}) %reduce-scatter.5.cloned.1.call-update) | async-done | bytes 655376 | tf_op jit(solution)/shard_map/cond/branch_1_fun/reduce_scatter | solution.py:72
  314.4 1.6 fusion.13
  316.2 24.3 %all_to_all.10 = bf16[32,8,2048]{2,1,0:T(8,128)(2,1)S(1)} all-to-all(bf16[32,8,2048]{2,1,0:T(8,128)(2,1)S(1)} %bitcast.57), channel_id=1, replica_groups=mesh['dp'=8,'expert_0'=4,'expert_1'=4,'expert_2'=2] {'expert_0','expert_..., dimensions={0} | all-to-all | bytes 2097152 | tf_op jit(solution)/shard_map/all_to_all | solution.py:87
  340.5 1.5 fusion.18
  (32 shorter events, 0.7 us)
Async XLA Ops:
  6.5 2.0 copy-start
  6.5 139.5 %copy-start.1 = (f32[1,128]{1,0:T(1,128)S(1)}, f32[1,128]{1,0:T(1,128)}, u32[]{:S(2)}) copy-start(f32[1,128]{1,0:T(1,128)} %param.13) | copy-start | bytes 1540
  10.0 154.5 %all-to-all-start = ((bf16[32,8,2048]{2,1,0:T(8,128)(2,1)}), bf16[32,8,2048]{2,1,0:T(8,128)(2,1)S(1)}, u32[]{:S(2)}, u32[]{:S(2)}) async-start(bf16[32,8,2048]{2,1,0:T(8,128)(2,1)} %fusion.19), calls=%async_computation.2 | async-start | bytes 2097152 | tf_op jit(solution)/shard_map/all_to_all | solution.py:33
  164.5 68.8 %all-gather.5.cloned.1.call-start = ((), (), s32[]{:S(2)}) async-start(), calls=%async_computation.6 | async-start | bytes 5898240 | tf_op jit(solution)/shard_map/cond/branch_1_fun/all_gather | solution.py:67
  166.0 148.4 %reduce-scatter.5.cloned.1.call-start = ((), (), s32[]{:S(2)}) async-start(), calls=%async_computation.7 | async-start | bytes 5898240 | tf_op jit(solution)/shard_map/cond/branch_1_fun/reduce_scatter | solution.py:72
Sparse Core Ops, SparseCore 0:
  167.1 66.1 all-gather.4
  250.4 63.9 reduce-scatter.4
where the time goes:
time: 349 us
  blocking collectives  168 us (48%)
  waiting for transfers between devices  129 us (37%)
  matrix products  22.7 us (7%)
  between operations  14.2 us (4%)
  starting transfers between devices  8.84 us (3%)
    psum x1, blocking collectives, on_device(): lax.psum(table.reshape(-1, LANES), EXPERT)  127 us
    all_gather x1, waiting for transfers between devices, experts(): slot_rows = lax.all_gather(plane, 'dp', axis=0, tiled=True)  67.1 us
    reduce_scatter x1, waiting for transfers between devices, experts(): lax.psum_scatter(share.astype(jnp.bfloat16), 'dp', scatter_dimension=0, t...  62.3 us
    all_to_all x1, blocking collectives, on_device(): lax.all_to_all(sent_back.reshape(expert_count, MOST, width), EXPERT, spli...  24.3 us
    dot_general x1, matrix products, experts(): share = jnp.dot(hidden, weight_out[0], preferred_element_type=jnp.float32)  16.9 us
    psum x1, blocking collectives, on_device(): both = lax.psum(both, 'dp')  16.5 us
    all_to_all x1, starting transfers between devices, on_device(): lax.all_to_all(packed.reshape(expert_count, MOST, width), EXPERT, split_a...  8.58 us
  transfers between devices with their start and end apart: 3, of which 2 were waited for; matrix products, arithmetic and copies ran while one was open for 1% of the time, Pallas kernels for 0%

commit v1 on v0

--- a/solution.py
+++ b/solution.py
@@ -36,7 +36,9 @@
     device_ids = lax.broadcasted_iota(jnp.int32, (expert_count, expert_count), 0)
     expert_ids = lax.broadcasted_iota(jnp.int32, (expert_count, expert_count), 1)
     table = jnp.where(device_ids == own_expert, counts[None, :], 0)
-    table = lax.psum(table.reshape(-1, LANES), EXPERT).reshape(expert_count, expert_count)
+    table = lax.psum(
+        lax.psum(table.reshape(-1, LANES), ("expert_1", "expert_2")), "expert_0"
+    ).reshape(expert_count, expert_count)
     arrived = jnp.sum(jnp.where(expert_ids == own_expert, table, 0), axis=1)
     plane_ids = lax.broadcasted_iota(jnp.int32, (dp_count, LANES), 0)
     lane_ids = lax.broadcasted_iota(jnp.int32, (dp_count, LANES), 1)

time: 349 us -> 252 us (0.72)
  blocking collectives: 168 us -> 70.6 us
    psum x1 -> x2, blocking collectives: 127 us -> 29.8 us  [the longest x1 18.2 us: on_device(): lax.psum(lax.psum(table.reshape(-1, LANES), ('expert_1', 'expert_2')), 'e...]
where the time goes in v1:
time: 252 us
  waiting for transfers between devices  130 us (52%)
  blocking collectives  70.6 us (28%)
  matrix products  22.7 us (9%)
  between operations  14.2 us (6%)
  starting transfers between devices  8.84 us (4%)
  other arithmetic  2.95 us (1%)
    all_gather x1, waiting for transfers between devices, experts(): slot_rows = lax.all_gather(plane, 'dp', axis=0, tiled=True)  67.2 us
    reduce_scatter x1, waiting for transfers between devices, experts(): lax.psum_scatter(share.astype(jnp.bfloat16), 'dp', scatter_dimension=0, t...  62.3 us
    all_to_all x1, blocking collectives, on_device(): lax.all_to_all(sent_back.reshape(expert_count, MOST, width), EXPERT, spli...  24.3 us
    psum x1, blocking collectives, on_device(): lax.psum(lax.psum(table.reshape(-1, LANES), ('expert_1', 'expert_2')), 'e...  18.2 us
    dot_general x1, matrix products, experts(): share = jnp.dot(hidden, weight_out[0], preferred_element_type=jnp.float32)  16.9 us
    psum x1, blocking collectives, on_device(): both = lax.psum(both, 'dp')  16.5 us
    psum x1, blocking collectives, on_device(): lax.psum(table.reshape(-1, LANES), ('expert_1', 'expert_2'))  11.6 us
    all_to_all x1, starting transfers between devices, on_device(): lax.all_to_all(packed.reshape(expert_count, MOST, width), EXPERT, split_a...  8.58 us
  transfers between devices with their start and end apart: 3, of which 2 were waited for; matrix products, arithmetic and copies ran while one was open for 1% of the time, Pallas kernels for 0%

profile of v1, /device:TPU:1, one launch (start us, length us, event | category | flops | bytes accessed | tf_op | source)
XLA Modules:
  0.0 251.7 jit_solution(13561348546763715642)
XLA Ops:
  6.5 0.9 convert_bitcast_fusion.1
  7.5 0.6 reduce-window.18
  8.1 0.2 slice_reduce_fusion
  8.3 0.1 iota.90
  8.4 0.1 convert_subtract_fusion
  8.5 1.5 fusion.19
  10.0 8.6 %all-to-all-start = ((bf16[32,8,2048]{2,1,0:T(8,128)(2,1)}), bf16[32,8,2048]{2,1,0:T(8,128)(2,1)S(1)}, u32[]{:S(2)}, u32[]{:S(2)}) async-start(bf16[32,8,2048]{2,1,0:T(8,128)(2,1)} %fusion.19), calls=%async_computation.2 | async-start | bytes 2097152 | tf_op jit(solution)/shard_map/all_to_all | solution.py:33
  18.7 0.1 iota.80
  18.9 11.6 %psum.21 = s32[8,128]{1,0:T(8,128)S(1)} all-reduce(s32[8,128]{1,0:T(8,128)S(1)} %broadcast_select_fusion.2), channel_id=1, replica_groups=mesh['dp'=8,'expert_0'=4,'expert_1'=4,'expert_2'=2] {'expert_1','expert_2'}, use_global_device_ids=true, to_apply=%region_3.4 | all-reduce | flops 1024 | bytes 8192 | tf_op jit(solution)/shard_map/psum | solution.py:40
  30.5 18.2 %psum.22 = s32[32,32]{1,0:T(8,128)S(1)} all-reduce(s32[32,32]{1,0:T(8,128)S(1)} %reshape.73), channel_id=1, replica_groups=mesh['dp'=8,'expert_0'=4,'expert_1'=4,'expert_2'=2] {'expert_0'}, use_global_device_ids=true, to_apply=%region_4.5 | all-reduce | flops 1024 | bytes 8192 | tf_op jit(solution)/shard_map/psum | solution.py:39
  48.7 0.1 select_reduce_fusion
  49.0 16.5 %psum.23 = f32[16,128]{1,0:T(8,128)S(1)} all-reduce(f32[16,128]{1,0:T(8,128)S(1)} %pad_maximum_fusion), channel_id=1, replica_groups=mesh['dp'=8,'expert_0'=4,'expert_1'=4,'expert_2'=2] {'dp'}, use_global_device_ids=true, to_apply=%region_6.7 | all-reduce | flops 2048 | bytes 16384 | tf_op jit(solution)/shard_map/psum | solution.py:52
  65.5 0.8 select_reduce_fusion.1
  67.0 0.1 copy.19
  67.1 0.1 reduce.1
  67.4 151.8 %conditional.2 = (bf16[256,2048]{1,0:T(8,128)(2,1)S(1)}) conditional(s32[]{:T(128)} %convert_element_type.61, (s32[32,8]{1,0:T(8,128)S(1)}, s32[]{:T(128)}, f32[1280]{0:T(1024)S(1)}, bf16[256,2048]{1,0:T(8,128)(2,1)S(1)}, bf16[1,2048,1024]{2,1,0:T(8,128)(2,1)}, /*index=5*/bf16[1,1024,2048]{2,1,0:T(8,128)(2,1)}) %tuple.30, (s32[32,8]{1,0:T(8,128)S(1)}, ...), branch_computations={%region_11.13_spmd, %region_13.15_spmd} | conditional | flops 17727356928 | bytes 85990520
  67.5 1.3 convolution_convert_fusion.3
  68.8 0.2 reduce-scatter.5.cloned.1.call-start
  69.1 67.2 %all-gather.5.cloned.1.call-done = bf16[1280,2048]{1,0:T(8,128)(2,1)} async-done(((bf16[160,2048]{1,0:T(8,128)(2,1)}), bf16[1280,2048]{1,0:T(8,128)(2,1)}) %all-gather.5.cloned.1.call-update) | async-done | bytes 5242896 | tf_op jit(solution)/shard_map/cond/branch_1_fun/all_gather | solution.py:69
  136.3 16.9 %convolution_convert_fusion.2 = bf16[1280,2048]{1,0:T(8,128)(2,1)} fusion(bf16[1,1024,2048]{2,1,0:T(8,128)(2,1)} %get-tuple-element.45, bf16[1280,2048]{1,0:T(8,128)(2,1)} %all-gather.5.cloned.1.call-done, bf16[1,2048,1024]{2,1,0:T(8,128)(2,1)} %get-tuple-element.44), kind=kOutput, calls=%fused_computation.13 | convolution fusion | flops 10742661120 | bytes 18874368 | tf_op jit(solution)/shard_map/cond/branch_1_fun/dot_general | solution.py:73
  155.0 62.3 %reduce-scatter.5.cloned.1.call-done = bf16[160,2048]{1,0:T(8,128)(2,1)} async-done(((bf16[1280,2048]{1,0:T(8,128)(2,1)}), bf16[160,2048]{1,0:T(8,128)(2,1)}) %reduce-scatter.5.cloned.1.call-update) | async-done | bytes 655376 | tf_op jit(solution)/shard_map/cond/branch_1_fun/reduce_scatter | solution.py:74
  217.3 1.6 fusion.13
  219.1 24.3 %all_to_all.10 = bf16[32,8,2048]{2,1,0:T(8,128)(2,1)S(1)} all-to-all(bf16[32,8,2048]{2,1,0:T(8,128)(2,1)S(1)} %bitcast.57), channel_id=1, replica_groups=mesh['dp'=8,'expert_0'=4,'expert_1'=4,'expert_2'=2] {'expert_0','expert_..., dimensions={0} | all-to-all | bytes 2097152 | tf_op jit(solution)/shard_map/all_to_all | solution.py:89
  243.4 1.5 fusion.18
  (33 shorter events, 0.8 us)
Async XLA Ops:
  6.5 2.0 copy-start
  6.5 42.4 %copy-start.1 = (f32[1,128]{1,0:T(1,128)S(1)}, f32[1,128]{1,0:T(1,128)}, u32[]{:S(2)}) copy-start(f32[1,128]{1,0:T(1,128)} %param.13) | copy-start | bytes 1540
  10.0 57.4 %all-to-all-start = ((bf16[32,8,2048]{2,1,0:T(8,128)(2,1)}), bf16[32,8,2048]{2,1,0:T(8,128)(2,1)S(1)}, u32[]{:S(2)}, u32[]{:S(2)}) async-start(bf16[32,8,2048]{2,1,0:T(8,128)(2,1)} %fusion.19), calls=%async_computation.2 | async-start | bytes 2097152 | tf_op jit(solution)/shard_map/all_to_all | solution.py:33
  67.4 68.9 %all-gather.5.cloned.1.call-start = ((), (), s32[]{:S(2)}) async-start(), calls=%async_computation.6 | async-start | bytes 5898240 | tf_op jit(solution)/shard_map/cond/branch_1_fun/all_gather | solution.py:69
  68.8 148.5 %reduce-scatter.5.cloned.1.call-start = ((), (), s32[]{:S(2)}) async-start(), calls=%async_computation.7 | async-start | bytes 5898240 | tf_op jit(solution)/shard_map/cond/branch_1_fun/reduce_scatter | solution.py:74
Sparse Core Ops, SparseCore 0:
  70.0 66.2 all-gather.4
  153.3 63.9 reduce-scatter.4
